TPU v7x, 32 devices: a whole 2x2x4 slice. The times are simulated.
32 devices in a mesh: seq: 8 (over z, x), res: 4 (over y, core).
Axes of the slice: x: 2, y: 2, z: 4, core: 2. Of those that a mesh axis runs over, the one named last changes fastest.
Arguments:
- alignment: bfloat16 [128, 4, 128, 256], P('seq', 'res'), may hold values from -8 to 8
- gain_attn: float32 [256], replicated, may hold values from 0.1 to 1.9
- w_proj: bfloat16 [256, 4, 256], replicated, may hold values from -0.75 to 0.75
- w_out: bfloat16 [256, 256], replicated, may hold values from -0.375 to 0.375
- gain_head: float32 [256], replicated, may hold values from 0.1 to 1.9
- w_head: bfloat16 [256, 23], replicated, may hold values from -1 to 1
- masked: int32 [128, 4, 128], P('res', None, 'seq'), may hold values from 0 to 1
- labels: int32 [128, 4, 128], P('res', None, 'seq'), may hold values from 0 to 22
Outputs:
- updated: bfloat16 [128, 4, 128, 256], P('res', None, 'seq')
- masked_loss: float32 [], replicated
- mask_share: float32 [], replicated
All inputs are finite; a program needn't handle non-finite values.
Results may differ from a plain program's by a relative error of at most 0.011.
Values may be sent and summed in bfloat16 or wider, within the bound.
A program may use at most 192 MiB of HBM per device.

v0:
```python
import jax
import jax.numpy as jnp
from jax import lax
from jax.sharding import PartitionSpec as P

HEADS = 8
HEAD_DIM = 32


def normalize(values, gain):
    mean = jnp.mean(values, axis=-1, keepdims=True)
    centred = values - mean
    spread = jnp.mean(centred * centred, axis=-1, keepdims=True)
    return centred * lax.rsqrt(spread + 1e-05) * gain


def project(flat_rows, gain_attn, w_proj):
    features = flat_rows.shape[1]
    normed = normalize(flat_rows.astype(jnp.float32), gain_attn).astype(jnp.bfloat16)
    return jnp.dot(
        normed, w_proj.reshape(features, 4 * features), preferred_element_type=jnp.float32
    ).astype(jnp.bfloat16)


def column_attention(queries, key_part, value_part):
    inv_root = HEAD_DIM ** (-0.5)
    scores = (
        jnp.einsum("shd,thd->hst", queries, key_part, preferred_element_type=jnp.float32) * inv_root
    )
    probs = jnp.exp(scores)
    totals = jnp.sum(probs, axis=2)
    weighted = jnp.einsum(
        "hst,thd->shd", probs.astype(jnp.bfloat16), value_part, preferred_element_type=jnp.float32
    )
    return (weighted, totals)


def finish(flat_rows, gated, w_out):
    summed = flat_rows.astype(jnp.float32) + jnp.dot(
        gated, w_out, preferred_element_type=jnp.float32
    )
    return summed.astype(jnp.bfloat16)


def on_device(alignment, gain_attn, w_proj, w_out, gain_head, w_head, masked, labels):
    weights = masked.reshape(-1).astype(jnp.float32)
    local_count = jnp.sum(weights)
    local_rows, single_block, segment, features = alignment.shape
    seq_devices = lax.axis_size("seq")
    split_view = alignment.reshape(local_rows, seq_devices, segment // seq_devices, features)
    column_block = lax.all_to_all(split_view, "seq", split_axis=1, concat_axis=0, tiled=True)
    seq_total, single, col_count, features = column_block.shape
    by_column = jnp.transpose(column_block.reshape(seq_total, col_count, features), (1, 0, 2))
    flat_rows = by_column.reshape(col_count * seq_total, features)
    projected = project(flat_rows, gain_attn, w_proj).reshape(
        col_count, seq_total, 4, HEADS, HEAD_DIM
    )

    def per_column(picked):
        weighted, totals = column_attention(picked[:, 0], picked[:, 1], picked[:, 2])
        attended = weighted / totals.T[:, :, None]
        gated_col = attended * jax.nn.sigmoid(picked[:, 3].astype(jnp.float32))
        return gated_col.reshape(seq_total, features).astype(jnp.bfloat16)

    gated = lax.map(per_column, projected).reshape(col_count * seq_total, features)
    result = finish(flat_rows, gated, w_out).reshape(col_count, seq_total, features)
    result = jnp.transpose(result, (1, 0, 2)).reshape(seq_total, single, col_count, features)
    updated = lax.all_to_all(result, "res", split_axis=0, concat_axis=1, tiled=True)
    features = updated.shape[3]
    flat_out = updated.reshape(-1, features)
    head_in = normalize(flat_out.astype(jnp.float32), gain_head).astype(jnp.bfloat16)
    logits = jnp.einsum("rc,ck->kr", head_in, w_head, preferred_element_type=jnp.float32)
    log_total = jnp.log(jnp.sum(jnp.exp(logits), axis=0))
    classes = jnp.arange(logits.shape[0], dtype=jnp.int32)[:, None]
    picked = jnp.sum(jnp.where(classes == labels.reshape(1, -1), logits, 0.0), axis=0)
    errors = log_total - picked
    local_loss = jnp.sum(errors * weights)
    loss_sum, mask_count = lax.psum((local_loss, local_count), ("seq", "res"))
    entries = flat_out.shape[0] * lax.axis_size("seq") * lax.axis_size("res")
    masked_loss = loss_sum / (1.0 + mask_count)
    mask_share = mask_count / entries
    return (updated, masked_loss, mask_share)


def solution(mesh):
    in_specs = (
        P("seq", "res", None, None),
        P(),
        P(),
        P(),
        P(),
        P(),
        P("res", None, "seq"),
        P("res", None, "seq"),
    )
    out_specs = (P("res", None, "seq", None), P(), P())
    return jax.shard_map(
        on_device, mesh=mesh, in_specs=in_specs, out_specs=out_specs, check_vma=False
    )
```

profile of v0, /device:TPU:12, one launch (start us, length us, event | category | flops | bytes accessed | tf_op | source)
XLA Modules:
  0.0 152.1 jit_solution(10787070603162363327)
XLA Ops:
  0.7 2.4 %copy.61 = bf16[16,8,16,256]{3,2,0,1:T(8,128)(2,1)} copy(bf16[16,8,16,256]{3,2,1,0:T(8,128)(2,1)} %bitcast.113) | data formatting | bytes 2097152 | tf_op jit(solution)/shard_map/reshape | solution.py:50
  3.0 6.3 %all-to-all-start = ((bf16[16,8,16,256]{3,2,0,1:T(8,128)(2,1)}), bf16[16,8,16,256]{3,2,0,1:T(8,128)(2,1)S(1)}, u32[]{:S(2)}, u32[]{:S(2)}) async-start(bf16[16,8,16,256]{3,2,0,1:T(8,128)(2,1)} %copy.61), calls=%async_computation | async-start | bytes 2097152 | tf_op jit(solution)/shard_map/all_to_all | solution.py:51
  9.4 23.3 %all-to-all-done = bf16[16,8,16,256]{3,2,0,1:T(8,128)(2,1)S(1)} async-done(((bf16[16,8,16,256]{3,2,0,1:T(8,128)(2,1)}), bf16[16,8,16,256]{3,2,0,1:T(8,128)(2,1)S(1)}, u32[]{:S(2)}, u32[]{:S(2)}) %all-to-all-start) | async-done | bytes 1048608 | tf_op jit(solution)/shard_map/all_to_all | solution.py:51
  32.9 1.2 bitcast_reduce_fusion
  34.1 1.2 copy.62
  35.3 1.6 %multiply_reduce_fusion.1 = f32[16,128]{1,0:T(8,128)S(1)} fusion(f32[16,128]{1,0:T(8,128)S(1)} %broadcast_multiply_fusion.1, f32[128,16,256]{2,1,0:T(8,128)S(1)} %bitcast.100), kind=kLoop, calls=%fused_computation.24 | loop fusion | flops 1570816 | bytes 2113536 | tf_op jit(solution)/shard_map/reduce_sum | solution.py:13
  37.0 1.4 multiply_convert_fusion
  38.3 3.2 %convolution_convert_fusion = bf16[2048,1024]{1,0:T(8,128)(2,1)} fusion(bf16[2048,256]{1,0:T(8,128)(2,1)S(1)} %bitcast.109, bf16[256,1024]{1,0:T(8,128)(2,1)S(1)} %bitcast.111), kind=kOutput, calls=%fused_computation.12 | convolution fusion | flops 1075838976 | bytes 5767168 | tf_op jit(solution)/shard_map/dot_general | solution.py:20
  41.5 6.5 %copy.63 = bf16[2048,1024]{0,1:T(8,128)(2,1)} copy(bf16[2048,1024]{1,0:T(8,128)(2,1)} %convolution_convert_fusion) | data formatting | bytes 8388608 | tf_op jit(solution)/shard_map/convert_element_type | solution.py:22
  48.0 3.6 %copy.80 = bf16[128,8,16,128]{3,2,1,0:T(8,128)(2,1)S(1)} copy(bf16[128,8,16,128]{3,1,2,0:T(8,128)(2,1)} %bitcast.106) | data formatting | bytes 8388608
  51.6 3.0 %copy.64 = bf16[16,128,4,8,32]{1,4,3,2,0:T(8,128)(2,1)} copy(bf16[16,128,4,8,32]{1,0,4,3,2:T(8,128)(2,1)S(1)} %bitcast.107) | data formatting | bytes 8388608 | tf_op jit(solution)/shard_map/while | solution.py:65
  54.7 26.1 %while.10 = (s32[]{:T(128)}, bf16[16,128,256]{2,1,0:T(8,128)(2,1)S(1)}, bf16[16,128,4,8,32]{1,4,3,2,0:T(8,128)(2,1)}, s32[]{:T(128)}) while((s32[]{:T(128)}, bf16[16,128,256]{2,1,0:T(8,128)(2,1)S(1)}, bf16[16,128,4,8,32]{1,4,3,2,0:T(8,128)(2,1)}, s32[]{:T(128)}) %tuple.42), condition=%wide.region_4.0_spmd, body=%wide.region_2.4_spmd.sunk | while | flops 17398784 | bytes 1646653 | solution.py:65
  56.3 1.0 dynamic-slice_bitcast_fusion.2
  57.9 1.0 dynamic-slice_bitcast_fusion.2
  61.2 1.0 dynamic-slice_bitcast_fusion.2
  67.7 1.0 dynamic-slice_bitcast_fusion.2
  69.4 1.0 dynamic-slice_bitcast_fusion.2
  72.6 1.0 dynamic-slice_bitcast_fusion.2
  81.3 1.6 %copy.85 = bf16[16,128,256]{2,0,1:T(8,128)(2,1)} copy(bf16[16,128,256]{2,1,0:T(8,128)(2,1)S(1)} %bitcast.110) | data formatting | bytes 2097152 | tf_op jit(solution)/shard_map/reshape | solution.py:66
  82.8 4.0 %all-to-all-start.1 = ((bf16[128,1,16,256]{3,2,1,0:T(8,128)(2,1)}), bf16[128,1,16,256]{3,2,1,0:T(8,128)(2,1)S(1)}, u32[]{:S(2)}, u32[]{:S(2)}) async-start(bf16[128,1,16,256]{3,2,1,0:T(8,128)(2,1)} %bitcast.79), calls=%async_computation.1 | async-start | bytes 2097152 | tf_op jit(solution)/shard_map/all_to_all | solution.py:68
  87.1 12.5 %all-to-all-done.1 = bf16[128,1,16,256]{3,2,1,0:T(8,128)(2,1)S(1)} async-done(((bf16[128,1,16,256]{3,2,1,0:T(8,128)(2,1)}), bf16[128,1,16,256]{3,2,1,0:T(8,128)(2,1)S(1)}, u32[]{:S(2)}, u32[]{:S(2)}) %all-to-all-start.1) | async-done | bytes 1048608 | tf_op jit(solution)/shard_map/all_to_all | solution.py:68
  102.5 1.1 exponential_reduce_fusion
  104.4 42.4 %all-reduce = (f32[]{:T(128)}, f32[]{:T(128)}) all-reduce(f32[]{:T(128)} %get-tuple-element.57, f32[]{:T(128)} %get-tuple-element.56), channel_id=1, replica_groups=mesh['seq'=8,'res'=4] {'seq','res'}, use_global_device_ids=true, to_apply=%region_10.11 | all-reduce | flops 2 | bytes 16 | tf_op jit(solution)/shard_map/psum | solution.py:78
  148.1 1.1 copy.75
  (113 shorter events, 24.3 us)
Async XLA Ops:
  0.6 80.2 %copy-start = (bf16[256,256]{1,0:T(8,128)(2,1)S(1)}, bf16[256,256]{1,0:T(8,128)(2,1)}, u32[]{:S(2)}) copy-start(bf16[256,256]{1,0:T(8,128)(2,1)} %param.13) | copy-start | bytes 393220
  0.6 8.6 %copy-start.2 = (bf16[256,4,256]{2,1,0:T(4,128)(2,1)S(1)}, bf16[256,4,256]{2,1,0:T(4,128)(2,1)}, u32[]{:S(2)}) copy-start(bf16[256,4,256]{2,1,0:T(4,128)(2,1)} %param.12) | copy-start | bytes 1572868
  3.0 29.6 %all-to-all-start = ((bf16[16,8,16,256]{3,2,0,1:T(8,128)(2,1)}), bf16[16,8,16,256]{3,2,0,1:T(8,128)(2,1)S(1)}, u32[]{:S(2)}, u32[]{:S(2)}) async-start(bf16[16,8,16,256]{3,2,0,1:T(8,128)(2,1)} %copy.61), calls=%async_computation | async-start | bytes 2097152 | tf_op jit(solution)/shard_map/all_to_all | solution.py:51
  35.3 1.7 %copy-start.5 = (f32[256]{0:T(256)S(1)}, f32[256]{0:T(256)}, u32[]{:S(2)}) copy-start(f32[256]{0:T(256)} %param.11) | copy-start | bytes 3076
  51.6 3.0 %copy-start.1 = (bf16[16,128,256]{2,1,0:T(8,128)(2,1)S(1)}, bf16[16,128,256]{2,1,0:T(8,128)(2,1)}, u32[]{:S(2)}) copy-start(bf16[16,128,256]{2,1,0:T(8,128)(2,1)} %custom-call) | copy-start | bytes 3145732
  81.3 5.6 %copy-start.3 = (s32[32,4,16]{0,2,1:T(8,128)S(1)}, s32[32,4,16]{0,2,1:T(8,128)}, u32[]{:S(2)}) copy-start(s32[32,4,16]{0,2,1:T(8,128)} %param.17) | copy-start | bytes 24580
  81.3 5.7 %copy-start.4 = (s32[32,4,16]{0,2,1:T(8,128)S(1)}, s32[32,4,16]{0,2,1:T(8,128)}, u32[]{:S(2)}) copy-start(s32[32,4,16]{0,2,1:T(8,128)} %param.16) | copy-start | bytes 24580
  82.8 16.8 %all-to-all-start.1 = ((bf16[128,1,16,256]{3,2,1,0:T(8,128)(2,1)}), bf16[128,1,16,256]{3,2,1,0:T(8,128)(2,1)S(1)}, u32[]{:S(2)}, u32[]{:S(2)}) async-start(bf16[128,1,16,256]{3,2,1,0:T(8,128)(2,1)} %bitcast.79), calls=%async_computation.1 | async-start | bytes 2097152 | tf_op jit(solution)/shard_map/all_to_all | solution.py:68
  100.2 1.4 copy-start.6
where the time goes:
time: 153 us; the launch traced here: 152 us
  blocking collectives  42.4 us (28%)
  local copies, waits for them, and re-layouts  38.2 us (25%)
  waiting for transfers between devices  35.8 us (23%)
  matrix products  12.7 us (8%)
  starting transfers between devices  10.2 us (7%)
  other arithmetic  7 us (5%)
  between operations  5.09 us (3%)
    psum x1, blocking collectives, on_device(): loss_sum, mask_count = lax.psum((local_loss, local_count), ('seq', 'res'))  42.4 us
    all_to_all x1, waiting for transfers between devices, on_device(): lax.all_to_all(split_view, 'seq', split_axis=1, concat_axis=0, tiled=True)  23.3 us
    squeeze x16, local copies, waits for them, and re-layouts, on_device(): lax.map(per_column, projected).reshape(col_count * seq_total, features)  15.5 us
    all_to_all x1, waiting for transfers between devices, on_device(): lax.all_to_all(result, 'res', split_axis=0, concat_axis=1, tiled=True)  12.5 us
    convert_element_type x1, local copies, waits for them, and re-layouts, project(): return jnp.dot(normed, w_proj.reshape(features, 4 * features), preferred_...  6.52 us
    all_to_all x1, starting transfers between devices, on_device(): lax.all_to_all(split_view, 'seq', split_axis=1, concat_axis=0, tiled=True)  6.25 us
    dot_general x16, matrix products, column_attention(): jnp.einsum('shd,thd->hst', queries, key_part, preferred_element_type=jnp....  5.03 us
    unnamed x19, local copies, waits for them, and re-layouts  4.99 us
  transfers between devices with their start and end apart: 2, of which 2 were waited for; matrix products, arithmetic and copies ran while one was open for 0% of the time, Pallas kernels for 0%

commit v1 on v0

--- a/solution.py
+++ b/solution.py
@@ -5,6 +5,10 @@
 
 HEADS = 8
 HEAD_DIM = 32
+
+
+def place_series_all(inp):
+    return lax.psum(lax.psum(inp, axis_name="res"), axis_name="seq")
 
 
 def normalize(values, gain):
@@ -75,7 +79,7 @@
     picked = jnp.sum(jnp.where(classes == labels.reshape(1, -1), logits, 0.0), axis=0)
     errors = log_total - picked
     local_loss = jnp.sum(errors * weights)
-    loss_sum, mask_count = lax.psum((local_loss, local_count), ("seq", "res"))
+    loss_sum, mask_count = place_series_all((local_loss, local_count))
     entries = flat_out.shape[0] * lax.axis_size("seq") * lax.axis_size("res")
     masked_loss = loss_sum / (1.0 + mask_count)
     mask_share = mask_count / entries

time: 153 us -> 142 us (0.928)
  the two profiles are of different devices: /device:TPU:12 before, /device:TPU:0 now
where the time goes in v1:
time: 142 us; the launch traced here: 141 us
  waiting for transfers between devices  39.6 us (28%)
  local copies, waits for them, and re-layouts  38.2 us (27%)
  blocking collectives  26.4 us (19%)
  matrix products  12.7 us (9%)
  starting transfers between devices  11 us (8%)
  other arithmetic  7 us (5%)
  between operations  5.11 us (4%)
    psum x2, blocking collectives, place_series_all(): return lax.psum(lax.psum(inp, axis_name='res'), axis_name='seq')  26.4 us
    all_to_all x1, waiting for transfers between devices, on_device(): lax.all_to_all(split_view, 'seq', split_axis=1, concat_axis=0, tiled=True)  25.7 us
    squeeze x16, local copies, waits for them, and re-layouts, on_device(): lax.map(per_column, projected).reshape(col_count * seq_total, features)  15.5 us
    all_to_all x1, waiting for transfers between devices, on_device(): lax.all_to_all(result, 'res', split_axis=0, concat_axis=1, tiled=True)  13.9 us
    all_to_all x1, starting transfers between devices, on_device(): lax.all_to_all(split_view, 'seq', split_axis=1, concat_axis=0, tiled=True)  7.28 us
    convert_element_type x1, local copies, waits for them, and re-layouts, project(): return jnp.dot(normed, w_proj.reshape(features, 4 * features), preferred_...  6.52 us
    dot_general x16, matrix products, column_attention(): jnp.einsum('shd,thd->hst', queries, key_part, preferred_element_type=jnp....  5.03 us
    unnamed x19, local copies, waits for them, and re-layouts  5 us
  transfers between devices with their start and end apart: 2, of which 2 were waited for; matrix products, arithmetic and copies ran while one was open for 0% of the time, Pallas kernels for 0%

profile of v1, /device:TPU:0, one launch (start us, length us, event | category | flops | bytes accessed | tf_op | source)
XLA Modules:
  0.0 140.7 jit_solution(9995308563212275326)
XLA Ops:
  0.7 2.4 %copy.61 = bf16[16,8,16,256]{3,2,0,1:T(8,128)(2,1)} copy(bf16[16,8,16,256]{3,2,1,0:T(8,128)(2,1)} %bitcast.113) | data formatting | bytes 2097152 | tf_op jit(solution)/shard_map/reshape | solution.py:54
  3.0 7.3 %all-to-all-start = ((bf16[16,8,16,256]{3,2,0,1:T(8,128)(2,1)}), bf16[16,8,16,256]{3,2,0,1:T(8,128)(2,1)S(1)}, u32[]{:S(2)}, u32[]{:S(2)}) async-start(bf16[16,8,16,256]{3,2,0,1:T(8,128)(2,1)} %copy.61), calls=%async_computation | async-start | bytes 2097152 | tf_op jit(solution)/shard_map/all_to_all | solution.py:55
  10.4 25.7 %all-to-all-done = bf16[16,8,16,256]{3,2,0,1:T(8,128)(2,1)S(1)} async-done(((bf16[16,8,16,256]{3,2,0,1:T(8,128)(2,1)}), bf16[16,8,16,256]{3,2,0,1:T(8,128)(2,1)S(1)}, u32[]{:S(2)}, u32[]{:S(2)}) %all-to-all-start) | async-done | bytes 1048608 | tf_op jit(solution)/shard_map/all_to_all | solution.py:55
  36.3 1.2 bitcast_reduce_fusion
  37.5 1.2 copy.62
  38.8 1.6 %multiply_reduce_fusion.1 = f32[16,128]{1,0:T(8,128)S(1)} fusion(f32[16,128]{1,0:T(8,128)S(1)} %broadcast_multiply_fusion.1, f32[128,16,256]{2,1,0:T(8,128)S(1)} %bitcast.100), kind=kLoop, calls=%fused_computation.24 | loop fusion | flops 1570816 | bytes 2113536 | tf_op jit(solution)/shard_map/reduce_sum | solution.py:17
  40.4 1.4 multiply_convert_fusion
  41.8 3.2 %convolution_convert_fusion = bf16[2048,1024]{1,0:T(8,128)(2,1)} fusion(bf16[2048,256]{1,0:T(8,128)(2,1)S(1)} %bitcast.109, bf16[256,1024]{1,0:T(8,128)(2,1)S(1)} %bitcast.111), kind=kOutput, calls=%fused_computation.12 | convolution fusion | flops 1075838976 | bytes 5767168 | tf_op jit(solution)/shard_map/dot_general | solution.py:24
  45.0 6.5 %copy.63 = bf16[2048,1024]{0,1:T(8,128)(2,1)} copy(bf16[2048,1024]{1,0:T(8,128)(2,1)} %convolution_convert_fusion) | data formatting | bytes 8388608 | tf_op jit(solution)/shard_map/convert_element_type | solution.py:26
  51.5 3.6 %copy.80 = bf16[128,8,16,128]{3,2,1,0:T(8,128)(2,1)S(1)} copy(bf16[128,8,16,128]{3,1,2,0:T(8,128)(2,1)} %bitcast.106) | data formatting | bytes 8388608
  55.1 3.0 %copy.64 = bf16[16,128,4,8,32]{1,4,3,2,0:T(8,128)(2,1)} copy(bf16[16,128,4,8,32]{1,0,4,3,2:T(8,128)(2,1)S(1)} %bitcast.107) | data formatting | bytes 8388608 | tf_op jit(solution)/shard_map/while | solution.py:69
  58.1 26.1 %while.10 = (s32[]{:T(128)}, bf16[16,128,256]{2,1,0:T(8,128)(2,1)S(1)}, bf16[16,128,4,8,32]{1,4,3,2,0:T(8,128)(2,1)}, s32[]{:T(128)}) while((s32[]{:T(128)}, bf16[16,128,256]{2,1,0:T(8,128)(2,1)S(1)}, bf16[16,128,4,8,32]{1,4,3,2,0:T(8,128)(2,1)}, s32[]{:T(128)}) %tuple.42), condition=%wide.region_4.0_spmd, body=%wide.region_2.4_spmd.sunk | while | flops 17398784 | bytes 1646653 | solution.py:69
  59.7 1.0 dynamic-slice_bitcast_fusion.2
  69.5 1.0 dynamic-slice_bitcast_fusion.2
  72.8 1.0 dynamic-slice_bitcast_fusion.2
  74.4 1.0 dynamic-slice_bitcast_fusion.2
  81.0 1.0 dynamic-slice_bitcast_fusion.2
  84.7 1.6 %copy.85 = bf16[16,128,256]{2,0,1:T(8,128)(2,1)} copy(bf16[16,128,256]{2,1,0:T(8,128)(2,1)S(1)} %bitcast.110) | data formatting | bytes 2097152 | tf_op jit(solution)/shard_map/reshape | solution.py:70
  86.3 3.7 %all-to-all-start.1 = ((bf16[128,1,16,256]{3,2,1,0:T(8,128)(2,1)}), bf16[128,1,16,256]{3,2,1,0:T(8,128)(2,1)S(1)}, u32[]{:S(2)}, u32[]{:S(2)}) async-start(bf16[128,1,16,256]{3,2,1,0:T(8,128)(2,1)} %bitcast.79), calls=%async_computation.1 | async-start | bytes 2097152 | tf_op jit(solution)/shard_map/all_to_all | solution.py:72
  90.3 13.9 %all-to-all-done.1 = bf16[128,1,16,256]{3,2,1,0:T(8,128)(2,1)S(1)} async-done(((bf16[128,1,16,256]{3,2,1,0:T(8,128)(2,1)}), bf16[128,1,16,256]{3,2,1,0:T(8,128)(2,1)S(1)}, u32[]{:S(2)}, u32[]{:S(2)}) %all-to-all-start.1) | async-done | bytes 1048608 | tf_op jit(solution)/shard_map/all_to_all | solution.py:72
  107.1 1.1 exponential_reduce_fusion
  109.0 6.4 %all-reduce.1 = (f32[]{:T(128)}, f32[]{:T(128)}) all-reduce(f32[]{:T(128)} %get-tuple-element.57, f32[]{:T(128)} %get-tuple-element.56), channel_id=1, replica_groups=mesh['seq'=8,'res'=4] {'res'}, use_global_device_ids=true, to_apply=%region_10.11 | all-reduce | flops 2 | bytes 16 | tf_op jit(solution)/shard_map/psum | solution.py:11
  115.3 20.1 %all-reduce = (f32[]{:T(128)}, f32[]{:T(128)}) all-reduce(f32[]{:T(128)} %get-tuple-element.66, f32[]{:T(128)} %get-tuple-element.67), channel_id=1, replica_groups=mesh['seq'=8,'res'=4] {'seq'}, use_global_device_ids=true, to_apply=%region_11.12 | all-reduce | flops 2 | bytes 16 | tf_op jit(solution)/shard_map/psum | solution.py:11
  136.7 1.1 copy.75
  (114 shorter events, 25.3 us)
Async XLA Ops:
  0.6 83.6 %copy-start = (bf16[256,256]{1,0:T(8,128)(2,1)S(1)}, bf16[256,256]{1,0:T(8,128)(2,1)}, u32[]{:S(2)}) copy-start(bf16[256,256]{1,0:T(8,128)(2,1)} %param.13) | copy-start | bytes 393220
  0.6 9.7 %copy-start.2 = (bf16[256,4,256]{2,1,0:T(4,128)(2,1)S(1)}, bf16[256,4,256]{2,1,0:T(4,128)(2,1)}, u32[]{:S(2)}) copy-start(bf16[256,4,256]{2,1,0:T(4,128)(2,1)} %param.12) | copy-start | bytes 1572868
  3.0 33.0 %all-to-all-start = ((bf16[16,8,16,256]{3,2,0,1:T(8,128)(2,1)}), bf16[16,8,16,256]{3,2,0,1:T(8,128)(2,1)S(1)}, u32[]{:S(2)}, u32[]{:S(2)}) async-start(bf16[16,8,16,256]{3,2,0,1:T(8,128)(2,1)} %copy.61), calls=%async_computation | async-start | bytes 2097152 | tf_op jit(solution)/shard_map/all_to_all | solution.py:55
  38.7 1.7 %copy-start.5 = (f32[256]{0:T(256)S(1)}, f32[256]{0:T(256)}, u32[]{:S(2)}) copy-start(f32[256]{0:T(256)} %param.11) | copy-start | bytes 3076
  55.1 3.0 %copy-start.1 = (bf16[16,128,256]{2,1,0:T(8,128)(2,1)S(1)}, bf16[16,128,256]{2,1,0:T(8,128)(2,1)}, u32[]{:S(2)}) copy-start(bf16[16,128,256]{2,1,0:T(8,128)(2,1)} %custom-call) | copy-start | bytes 3145732
  84.7 5.3 %copy-start.3 = (s32[32,4,16]{0,2,1:T(8,128)S(1)}, s32[32,4,16]{0,2,1:T(8,128)}, u32[]{:S(2)}) copy-start(s32[32,4,16]{0,2,1:T(8,128)} %param.17) | copy-start | bytes 24580
  84.7 5.5 %copy-start.4 = (s32[32,4,16]{0,2,1:T(8,128)S(1)}, s32[32,4,16]{0,2,1:T(8,128)}, u32[]{:S(2)}) copy-start(s32[32,4,16]{0,2,1:T(8,128)} %param.16) | copy-start | bytes 24580
  86.3 17.9 %all-to-all-start.1 = ((bf16[128,1,16,256]{3,2,1,0:T(8,128)(2,1)}), bf16[128,1,16,256]{3,2,1,0:T(8,128)(2,1)S(1)}, u32[]{:S(2)}, u32[]{:S(2)}) async-start(bf16[128,1,16,256]{3,2,1,0:T(8,128)(2,1)} %bitcast.79), calls=%async_computation.1 | async-start | bytes 2097152 | tf_op jit(solution)/shard_map/all_to_all | solution.py:72
  104.8 1.4 copy-start.6
